TPU v7x, 32 devices: a whole 2x2x4 slice. The times are simulated.
32 devices in a mesh: seq: 8 (over z, x), wsh: 4 (over y, core).
Axes of the slice: x: 2, y: 2, z: 4, core: 2. Of those that a mesh axis runs over, the one named last changes fastest.
Arguments:
- tokens_in: bfloat16 [4, 4096, 1024], P('wsh', 'seq'), may hold values from -6 to 6
- out_grad: bfloat16 [4, 4096, 1024], P('wsh', 'seq'), may hold values from -6 to 6
- deal_order: int32 [8], replicated, may hold values from 0 to 7, each once
- seq_lengths: int32 [4, 4], P('wsh'), may hold values from 1 to 2048, 4096 in all within a row
- weights: bfloat16 [1024, 17920], P('wsh'), may hold values from -0.1875 to 0.1875
- norm_gains: bfloat16 [2, 1024], P(None, 'wsh'), may hold values from 0.5 to 1.5
- conv_kernel: bfloat16 [3, 1024], P(None, 'wsh'), may hold values from -3 to 3
- vector_state: float32 [5, 1024], P(None, 'wsh'), may hold values from 0.2 to 5
- kron_stats: float32 [2, 1120, 128, 128], P(None, 'wsh', 'seq'), may hold values from -6 to 6
- kron_roots: float32 [2, 1120, 128, 128], P(None, 'wsh', 'seq'), as said below
Outputs:
- block_out: bfloat16 [4, 4096, 1024], P('wsh', 'seq')
- input_grad: bfloat16 [4, 4096, 1024], P('wsh', 'seq')
- weight_grad: float32 [1024, 17920], P('wsh')
- vector_grad: float32 [5, 1024], P(None, 'wsh')
- vector_state_new: float32 [5, 1024], P(None, 'wsh')
- vector_update: float32 [5, 1024], P(None, 'wsh')
- kron_stats_new: float32 [2, 1120, 128, 128], P(None, 'wsh', 'seq')
- weight_update: float32 [1120, 128, 128], P('wsh', 'seq')
Inputs may be any that keep to these rules, and one draw needn't show every extreme that they name: `deal_order`: a permutation of 0 to 7. `seq_lengths`: each row sums to 4096; in every pack the longest sequence has exactly 2048 tokens. `kron_roots`: each block has a dominant diagonal between 0.5 and 2.
All inputs are finite; a program needn't handle non-finite values.
Results may differ from a plain program's by a relative error of at most 0.025.
Values may be sent and summed in bfloat16 or wider, within the bound.
A program may use at most 320 MiB of HBM per device.

v0:
```python
import jax
import jax.numpy as jnp
from jax import lax
from jax.sharding import PartitionSpec as P

D = 1024
FF = 4608
BLK = 128
EPS = 1e-05
BETA = 0.5
BETA_VEC = 0.5
LEARN = 0.03
LEARN_VEC = 0.05
HIGH = lax.Precision.HIGHEST


def passed_along(block, axis, distance):
    devices = range(lax.axis_size(axis))
    route = [(i - distance, i) for i in devices if i - distance in devices]
    return lax.ppermute(block, axis, route)


def seq_positions(lengths_row, first, count):
    starts = jnp.cumsum(lengths_row) - lengths_row
    rows_at = first + jnp.arange(count, dtype=jnp.int32)
    begin = jnp.max(jnp.where(starts[None, :] <= rows_at[:, None], starts[None, :], 0), axis=1)
    return rows_at - begin


def rms_scale(values):
    return lax.rsqrt(jnp.mean(values * values, axis=1, keepdims=True) + EPS)


def norm_back(upstream, values, scale, gain):
    scaled = upstream * gain
    inner = jnp.mean(scaled * values, axis=1, keepdims=True)
    return (
        scale * scaled - values * scale * scale * scale * inner,
        jnp.sum(upstream * values * scale, axis=0),
    )


def contract_rows(left, right):
    return lax.dot_general(
        left, right, (((0,), (0,)), ((), ())), preferred_element_type=jnp.float32
    )


def contract_cols(left, right):
    return lax.dot_general(
        left, right, (((1,), (1,)), ((), ())), preferred_element_type=jnp.float32
    )


def shards(
    tokens_in,
    out_grad,
    deal_order,
    seq_lengths,
    weights,
    norm_gains,
    conv_kernel,
    vector_state,
    kron_stats,
    kron_roots,
):
    n_seq = lax.axis_size("seq")
    n_wsh = lax.axis_size("wsh")
    rows = tokens_in.shape[1]
    unit = rows // n_seq
    arrived = (
        lax.all_to_all(
            tokens_in.reshape(n_seq, unit, D), "seq", split_axis=0, concat_axis=0, tiled=True
        ),
        lax.all_to_all(
            out_grad.reshape(n_seq, unit, D), "seq", split_axis=0, concat_axis=0, tiled=True
        ),
    )
    x_bf = jnp.take(arrived[0], deal_order, axis=0).reshape(rows, D)
    dy_bf = jnp.take(arrived[1], deal_order, axis=0).reshape(rows, D)
    full_w, gains_bf, kernel_bf = (
        lax.all_gather(weights, "wsh", axis=0, tiled=True),
        lax.all_gather(norm_gains, "wsh", axis=1, tiled=True),
        lax.all_gather(conv_kernel, "wsh", axis=1, tiled=True),
    )
    gains = gains_bf.astype(jnp.float32)
    kernel = kernel_bf.astype(jnp.float32)
    first_row = lax.axis_index("seq") * rows
    pos = seq_positions(seq_lengths[0], first_row, rows + 2)
    masks = [(pos >= 2 - k).astype(jnp.float32)[:, None] for k in range(3)]
    xf = x_bf.astype(jnp.float32)
    scale_one = rms_scale(xf)
    xn = (xf * scale_one * gains[0]).astype(jnp.bfloat16)
    proj = jnp.dot(xn, full_w[:, : 3 * D], preferred_element_type=jnp.float32)
    b_part = proj[:, :D]
    c_part = proj[:, D : 2 * D]
    x_part = proj[:, 2 * D :]
    conv_in = b_part * x_part
    prev = passed_along(conv_in[rows - 2 :], "seq", 1)
    ext = jnp.concatenate([prev, conv_in], axis=0)
    conv = (
        kernel[0] * masks[0][:rows] * ext[0:rows]
        + kernel[1] * masks[1][:rows] * ext[1 : rows + 1]
        + kernel[2] * masks[2][:rows] * ext[2 : rows + 2]
    )
    yc = (c_part * conv).astype(jnp.bfloat16)
    hidden_sum = xf + jnp.dot(yc, full_w[:, 3 * D : 4 * D], preferred_element_type=jnp.float32)
    scale_two = rms_scale(hidden_sum)
    hn = (hidden_sum * scale_two * gains[1]).astype(jnp.bfloat16)
    gate_up = jnp.dot(hn, full_w[:, 4 * D : 4 * D + 2 * FF], preferred_element_type=jnp.float32)
    gate = gate_up[:, :FF]
    upper = gate_up[:, FF:]
    sig = jax.nn.sigmoid(gate)
    act = (gate * sig * upper).astype(jnp.bfloat16)
    ffn = contract_cols(act, full_w[:, 4 * D + 2 * FF :])
    result = (hidden_sum + ffn).astype(jnp.bfloat16)
    g_down = contract_rows(dy_bf, act)
    d_act = jnp.dot(dy_bf, full_w[:, 4 * D + 2 * FF :], preferred_element_type=jnp.float32)
    d_gate = d_act * upper * sig * (1.0 + gate * (1.0 - sig))
    d_upper = d_act * gate * sig
    d_gu = jnp.concatenate([d_gate, d_upper], axis=1).astype(jnp.bfloat16)
    g_gu = contract_rows(hn, d_gu)
    d_hn = contract_cols(d_gu, full_w[:, 4 * D : 4 * D + 2 * FF])
    d_norm_two, g_gain_two = norm_back(d_hn, hidden_sum, scale_two, gains[1])
    d_hidden = dy_bf.astype(jnp.float32) + d_norm_two
    d_mix = d_hidden.astype(jnp.bfloat16)
    g_out = contract_rows(yc, d_mix)
    d_yc = contract_cols(d_mix, full_w[:, 3 * D : 4 * D])
    d_c = d_yc * conv
    d_conv = d_yc * c_part
    after = passed_along(d_conv[:2], "seq", -1)
    d_ext = jnp.concatenate([d_conv, after], axis=0)
    weighted = [d_ext * masks[k] for k in range(3)]
    d_bx = (
        kernel[2] * weighted[2][:rows]
        + kernel[1] * weighted[1][1 : rows + 1]
        + kernel[0] * weighted[0][2 : rows + 2]
    )
    g_taps = jnp.stack([jnp.sum(weighted[k][:rows] * ext[k : k + rows], axis=0) for k in range(3)])
    d_proj = jnp.concatenate([d_bx * x_part, d_c, d_bx * b_part], axis=1).astype(jnp.bfloat16)
    g_in = contract_rows(xn, d_proj)
    d_xn = contract_cols(d_proj, full_w[:, : 3 * D])
    d_norm_one, g_gain_one = norm_back(d_xn, xf, scale_one, gains[0])
    d_input = (d_hidden + d_norm_one).astype(jnp.bfloat16)
    g_vec = jnp.concatenate([g_gain_one[None], g_gain_two[None], g_taps], axis=0)
    inverse = jnp.argsort(deal_order)
    leaving = (
        jnp.take(result.reshape(n_seq, unit, D), inverse, axis=0),
        jnp.take(d_input.reshape(n_seq, unit, D), inverse, axis=0),
    )
    returned = (
        lax.all_to_all(leaving[0], "seq", split_axis=0, concat_axis=0, tiled=True),
        lax.all_to_all(leaving[1], "seq", split_axis=0, concat_axis=0, tiled=True),
    )
    summed = (
        lax.psum_scatter(g_in.astype(jnp.bfloat16), "wsh", scatter_dimension=0, tiled=True).astype(
            jnp.float32
        ),
        lax.psum_scatter(g_out.astype(jnp.bfloat16), "wsh", scatter_dimension=0, tiled=True).astype(
            jnp.float32
        ),
        lax.psum_scatter(g_gu.astype(jnp.bfloat16), "wsh", scatter_dimension=0, tiled=True).astype(
            jnp.float32
        ),
        lax.psum_scatter(
            g_down.astype(jnp.bfloat16), "wsh", scatter_dimension=0, tiled=True
        ).astype(jnp.float32),
        lax.psum_scatter(g_vec.astype(jnp.bfloat16), "wsh", scatter_dimension=1, tiled=True).astype(
            jnp.float32
        ),
    )
    summed = (
        lax.psum(summed[0].astype(jnp.bfloat16), "seq").astype(jnp.float32),
        lax.psum(summed[1].astype(jnp.bfloat16), "seq").astype(jnp.float32),
        lax.psum(summed[2].astype(jnp.bfloat16), "seq").astype(jnp.float32),
        lax.psum(summed[3].astype(jnp.bfloat16), "seq").astype(jnp.float32),
        lax.psum(summed[4].astype(jnp.bfloat16), "seq").astype(jnp.float32),
    )
    grad_scale = lax.rsqrt(jnp.asarray(rows * n_seq * n_wsh, jnp.float32))
    grad_shard = jnp.concatenate([summed[0], summed[1], summed[2], summed[3]], axis=1) * grad_scale
    vec_grad = summed[4] * grad_scale
    state_new = BETA_VEC * vector_state + (1.0 - BETA_VEC) * vec_grad * vec_grad
    vec_update = -LEARN_VEC * vec_grad * lax.rsqrt(state_new)
    nrow_blocks = grad_shard.shape[0] // BLK
    ncol_blocks = grad_shard.shape[1] // BLK
    grad_blocks = (
        grad_shard.reshape(nrow_blocks, BLK, ncol_blocks, BLK)
        .transpose(0, 2, 1, 3)
        .reshape(nrow_blocks * ncol_blocks, BLK, BLK)
    )
    share = BLK // n_seq
    first_block_row = lax.axis_index("seq") * share
    block_rows = lax.dynamic_slice_in_dim(grad_blocks, first_block_row, share, 1)
    block_cols = lax.dynamic_slice_in_dim(grad_blocks, first_block_row, share, 2)
    left_term = jnp.einsum("nij,nkj->nik", block_rows, grad_blocks, precision=HIGH)
    right_term = jnp.einsum("nji,njk->nik", block_cols, grad_blocks, precision=HIGH)
    stats_new = jnp.stack(
        [
            BETA * kron_stats[0] + (1.0 - BETA) * left_term / BLK,
            BETA * kron_stats[1] + (1.0 - BETA) * right_term / BLK,
        ]
    )
    right_full = lax.all_gather(
        kron_roots[1].astype(jnp.bfloat16), "seq", axis=1, tiled=True
    ).astype(jnp.float32)
    left_mul = jnp.einsum("nij,njk->nik", kron_roots[0], grad_blocks, precision=HIGH)
    update = -LEARN * jnp.einsum("nij,njk->nik", left_mul, right_full, precision=HIGH)
    return (
        returned[0].reshape(1, rows, D),
        returned[1].reshape(1, rows, D),
        grad_shard,
        vec_grad,
        state_new,
        vec_update,
        stats_new,
        update,
    )


def solution(mesh):
    return jax.shard_map(
        shards,
        mesh=mesh,
        in_specs=(
            P("wsh", "seq", None),
            P("wsh", "seq", None),
            P(),
            P("wsh", None),
            P("wsh", None),
            P(None, "wsh"),
            P(None, "wsh"),
            P(None, "wsh"),
            P(None, "wsh", "seq", None),
            P(None, "wsh", "seq", None),
        ),
        out_specs=(
            P("wsh", "seq", None),
            P("wsh", "seq", None),
            P("wsh", None),
            P(None, "wsh"),
            P(None, "wsh"),
            P(None, "wsh"),
            P(None, "wsh", "seq", None),
            P("wsh", "seq", None),
        ),
        check_vma=False,
    )
```

profile of v0, /device:TPU:0, one launch (start us, length us, event | category | flops | bytes accessed | tf_op | source)
XLA Modules:
  0.0 1136.9 jit_solution(3107054169689322003)
XLA Ops:
  7.9 7.4 all-to-all-start
  15.6 25.6 %all-to-all-done = bf16[8,64,1024]{2,1,0:T(8,128)(2,1)S(1)} async-done(((bf16[8,64,1024]{2,1,0:T(8,128)(2,1)}), bf16[8,64,1024]{2,1,0:T(8,128)(2,1)S(1)}, u32[]{:S(2)}, u32[]{:S(2)}) %all-to-all-start) | async-done | bytes 1048608 | tf_op jit(solution)/shard_map/all_to_all | solution.py:72
  41.1 4.3 all-to-all-start.2
  45.6 5.2 all_gather.12
  50.8 5.3 all_gather.14
  57.4 13.6 %all-to-all-done.2 = bf16[8,64,1024]{2,1,0:T(8,128)(2,1)} async-done(((bf16[8,64,1024]{2,1,0:T(8,128)(2,1)}), bf16[8,64,1024]{2,1,0:T(8,128)(2,1)}, u32[]{:S(2)}, u32[]{:S(2)}) %all-to-all-start.2) | async-done | bytes 1048608 | tf_op jit(solution)/shard_map/all_to_all | solution.py:75
  71.0 2.8 gather_fusion.2
  74.1 159.7 %all-gather.4.cloned.1.call-done = bf16[1024,17920]{1,0:T(8,128)(2,1)} async-done(((bf16[256,17920]{1,0:T(8,128)(2,1)}), bf16[1024,17920]{1,0:T(8,128)(2,1)}) %all-gather.4.cloned.1.call-update) | async-done | bytes 36700176 | tf_op jit(solution)/shard_map/all_gather | solution.py:82
  233.8 5.5 fusion.14
  239.8 3.7 collective-permute-start
  244.7 2.3 multiply_convert_fusion.7
  247.0 3.3 multiply_reduce_fusion.3
  250.3 18.3 %fusion.4 = f32[512,9216]{1,0:T(8,128)} fusion(bf16[1024,17920]{1,0:T(8,128)(2,1)} %all-gather.4.cloned.1.call-done, f32[512,1024]{1,0:T(8,128)S(1)} %get-tuple-element.51, f32[1024]{0:T(1024)S(1)} %bitcast.99, f32[512]{0:T(512)S(1)} %add_rsqrt_fusion.1), kind=kOutput, calls=%fused_computation.10 | convolution fusion | flops 9665249280 | bytes 39852032 | tf_op jit(solution)/shard_map/dot_general | solution.py:110
  268.6 17.8 %multiply_convert_fusion.1 = (bf16[512,4608]{1,0:T(8,128)(2,1)}, bf16[512,4608]{1,0:T(8,128)(2,1)}, bf16[512,4608]{1,0:T(8,128)(2,1)}) fusion(f32[512,9216]{1,0:T(8,128)} %fusion.4, bf16[512,1024]{1,0:T(8,128)(2,1)} %bitcast.86, bf16[1024,17920]{1,0:T(8,128)(2,1)} %all-gather.4.cloned.1.call-done), kind=kOutput, calls=%fused_computation.15 | convolution fusion | flops 4869586944 | bytes 43515904 | tf_op jit(solution)/shard_map/dot_general | solution.py:118
  286.4 16.0 %multiply_reduce_fusion.1 = (bf16[1024]{0:T(1024)(128)(2,1)S(1)}, f32[512]{0:T(512)S(1)}, f32[512,1024]{1,0:T(8,128)S(1)}) fusion(f32[512,1024]{1,0:T(8,128)} %copy-done.10, f32[512]{0:T(512)S(1)} %add_rsqrt_fusion.1, f32[1024]{0:T(1024)S(1)} %bitcast.100, bf16[1024,17920]{1,0:T(8,128)(2,1)} %all-gather.4.cloned.1.call-done, ...), kind=kOutput, calls=%fused_computation.75 | convolution fusion | flops 9685694464 | bytes 32516096 | tf_op jit(solution)/shard_map/dot_general | solution.py:50
  303.2 1.5 copy-done.2
  304.7 2.6 convolution_convert_fusion.3
  307.4 3.7 fusion.42
  311.1 2.4 multiply_convert_fusion.4
  313.5 1.3 collective-permute-start.1
  314.8 4.5 collective-permute-done.1
  319.7 2.6 fusion.26
  324.2 5.7 convolution_convert_fusion.2
  331.1 9.8 convolution_convert_fusion.1
  341.0 1.5 copy-done.12
  342.6 17.8 %convolution_convert_fusion = bf16[1024,9216]{1,0:T(8,128)(2,1)} fusion(bf16[512,4608]{1,0:T(8,128)(2,1)} %get-tuple-element.32, bf16[512,4608]{1,0:T(8,128)(2,1)} %get-tuple-element.31, f32[512,1024]{1,0:T(8,128)S(1)} %copy-done.12, f32[1024]{0:T(1024)S(1)} %bitcast.102, f32[512]{0:T(512)S(1)} %add_rsqrt_fusion.1), kind=kOutput, calls=%fused_computation.7 | convolution fusion | flops 9693560832 | bytes 30414848 | tf_op jit(solution)/shard_map/dot_general | solution.py:44
  360.4 9.6 fusion.41
  370.8 30.0 %reduce-scatter.6.cloned.1.call-done = bf16[256,3072]{1,0:T(8,128)(2,1)} async-done(((bf16[1024,3072]{1,0:T(8,128)(2,1)}), bf16[256,3072]{1,0:T(8,128)(2,1)}) %reduce-scatter.6.cloned.1.call-update) | async-done | bytes 1572880 | tf_op jit(solution)/shard_map/reduce_scatter | solution.py:156
  400.9 81.0 %reduce-scatter.12.cloned.1.call-done = bf16[256,4608]{1,0:T(8,128)(2,1)} async-done(((bf16[1024,4608]{1,0:T(8,128)(2,1)}), bf16[256,4608]{1,0:T(8,128)(2,1)}) %reduce-scatter.12.cloned.1.call-update) | async-done | bytes 2359312 | tf_op jit(solution)/shard_map/reduce_scatter | solution.py:165
  481.9 140.3 %reduce-scatter.10.cloned.1.call-done = bf16[256,9216]{1,0:T(8,128)(2,1)} async-done(((bf16[1024,9216]{1,0:T(8,128)(2,1)}), bf16[256,9216]{1,0:T(8,128)(2,1)}) %reduce-scatter.10.cloned.1.call-update) | async-done | bytes 4718608 | tf_op jit(solution)/shard_map/reduce_scatter | solution.py:162
  622.3 2.8 slice.250
  626.1 9.9 add_convert_fusion
  636.0 3.0 gather_fusion.1
  638.9 3.3 fusion.37
  642.2 1.9 gather_fusion.3
  645.4 58.2 %all_to_all.20 = bf16[8,64,1024]{2,1,0:T(8,128)(2,1)S(1)} all-to-all(bf16[8,64,1024]{2,1,0:T(8,128)(2,1)S(1)} %get-tuple-element.49), channel_id=1, replica_groups=mesh['seq'=8,'wsh'=4] {'seq'}, dimensions={0} | all-to-all | bytes 2097152 | tf_op jit(solution)/shard_map/all_to_all | solution.py:152
  703.6 3.7 all-to-all-start.3
  707.3 49.4 %psum.39 = bf16[5,256]{1,0:T(8,128)(2,1)S(1)} all-reduce(bf16[5,256]{1,0:T(8,128)(2,1)} %reduce-scatter.14.cloned.1.call-done), channel_id=1, replica_groups=mesh['seq'=8,'wsh'=4] {'seq'}, use_global_device_ids=true, to_apply=%region_21.23 | all-reduce | flops 1280 | bytes 5120 | tf_op jit(solution)/shard_map/psum | solution.py:177
  758.3 222.7 %all-reduce.3.cloned.1.call-done = (bf16[256,4608]{1,0:T(8,128)(2,1)}, bf16[256,9216]{1,0:T(8,128)(2,1)}, bf16[256,1024]{1,0:T(8,128)(2,1)}, bf16[256,3072]{1,0:T(8,128)(2,1)}) async-done(((bf16[256,4608]{1,0:T(8,128)(2,1)}, bf16[256,9216]{1,0:T(8,128)(2,1)}, bf16[256,1024]{1,0:T(8,128)(2,1)}, bf16[256,3072]{1,0:T(8,128)(2,1)}), (bf16[256,4608]{1,0:T(8,128)(2,1)}, bf16[256,9216]{1,0:T(8,128)(2,1)}, ...) | async-done | bytes 9175056 | tf_op jit(solution)/shard_map/psum | solution.py:176
  980.9 10.2 convert_multiply_fusion
  991.1 19.2 %mul.433 = f32[2,128,140,128]{3,2,1,0:T(8,128)} reshape(f32[256,17920]{1,0:T(8,128)} %convert_multiply_fusion) | data formatting | bytes 36700160 | tf_op jit(solution)/shard_map/mul | solution.py:180
  1010.3 12.0 %copy.22 = f32[2,140,128,128]{3,2,1,0:T(8,128)S(1)} copy(f32[2,140,128,128]{3,1,2,0:T(8,128)} %bitcast.79) | data formatting | bytes 36700160 | tf_op jit(solution)/shard_map/transpose | solution.py:188
  1022.4 29.2 %fusion.19 = f32[1,280,16,128]{3,2,1,0:T(8,128)S(1)} fusion(f32[2,280,16,128]{3,2,1,0:T(8,128)S(1)} %bitcast.83, f32[280,128,128]{2,1,0:T(8,128)S(1)} %bitcast.76, s32[]{:T(128)S(6)} %select_n.16), kind=kOutput, calls=%fused_computation.39 | convolution fusion | flops 882524160 | bytes 25231364 | tf_op jit(solution)/shard_map/nij,nkj->nik/dot_general | solution.py:195
  1051.6 35.4 %fusion.18 = f32[1,280,16,128]{3,2,1,0:T(8,128)S(1)} fusion(f32[2,280,16,128]{3,2,1,0:T(8,128)S(1)} %bitcast.83, f32[280,128,128]{2,1,0:T(8,128)S(1)} %bitcast.77, s32[]{:T(128)S(6)} %select_n.16), kind=kOutput, calls=%fused_computation.37 | convolution fusion | flops 882524160 | bytes 41287684 | tf_op jit(solution)/shard_map/nji,njk->nik/dot_general | solution.py:196
  1087.0 2.4 pad_maximum_fusion.3
  1089.5 17.0 %fusion.16 = f32[280,128,16]{1,2,0:T(8,128)S(1)} fusion(f32[280,128,128]{2,1,0:T(8,128)S(1)} %bitcast.78, f32[2,280,16,128]{3,2,1,0:T(8,128)} %param.21), kind=kOutput, calls=%fused_computation.34 | convolution fusion | flops 880803840 | bytes 22937600 | tf_op jit(solution)/shard_map/nij,njk->nik/dot_general | solution.py:206
  1106.5 10.2 all-gather.6.cloned.1.call-done
  1116.6 10.6 fusion.54
  (121 shorter events, 15.8 us)
Async XLA Ops:
  7.2 8.2 copy-start.23
  7.2 226.6 %all-gather.4.cloned.1.call-start = ((), (), s32[]{:S(2)}) async-start(), calls=%async_computation.9 | async-start | bytes 45875200 | tf_op jit(solution)/shard_map/all_gather | solution.py:82
  7.9 37.7 %copy-start.22 = (bf16[2,256]{1,0:T(2,128)(2,1)S(1)}, bf16[2,256]{1,0:T(2,128)(2,1)}, u32[]{:S(2)}) copy-start(bf16[2,256]{1,0:T(2,128)(2,1)} %param.17) | copy-start | bytes 3076
  7.9 42.9 %copy-start.21 = (bf16[3,256]{1,0:T(4,128)(2,1)S(1)}, bf16[3,256]{1,0:T(4,128)(2,1)}, u32[]{:S(2)}) copy-start(bf16[3,256]{1,0:T(4,128)(2,1)} %param.18) | copy-start | bytes 4612
  7.9 48.2 %copy-start.24 = (s32[8]{0:T(128)S(1)}, s32[8]{0:T(128)}, u32[]{:S(2)}) copy-start(s32[8]{0:T(128)} %param.14) | copy-start | bytes 100
  7.9 33.2 %all-to-all-start = ((bf16[8,64,1024]{2,1,0:T(8,128)(2,1)}), bf16[8,64,1024]{2,1,0:T(8,128)(2,1)S(1)}, u32[]{:S(2)}, u32[]{:S(2)}) async-start(bf16[8,64,1024]{2,1,0:T(8,128)(2,1)} %bitcast), calls=%async_computation | async-start | bytes 2097152 | tf_op jit(solution)/shard_map/all_to_all | solution.py:72
  41.1 29.8 %all-to-all-start.2 = ((bf16[8,64,1024]{2,1,0:T(8,128)(2,1)}), bf16[8,64,1024]{2,1,0:T(8,128)(2,1)}, u32[]{:S(2)}, u32[]{:S(2)}) async-start(bf16[8,64,1024]{2,1,0:T(8,128)(2,1)} %bitcast.10), calls=%async_computation.2 | async-start | bytes 2097152 | tf_op jit(solution)/shard_map/all_to_all | solution.py:75
  45.4 325.4 %reduce-scatter.8.cloned.1.call-start = ((), (), s32[]{:S(2)}) async-start(), calls=%async_computation.11 | async-start | bytes 2621440 | tf_op jit(solution)/shard_map/reduce_scatter | solution.py:159
  74.1 159.7 %copy-start.18 = (bf16[512,1024]{1,0:T(8,128)(2,1)}, bf16[512,1024]{1,0:T(8,128)(2,1)S(1)}, u32[]{:S(2)}) copy-start(bf16[512,1024]{1,0:T(8,128)(2,1)S(1)} %fusion.32) | copy-start | bytes 3145732
  239.3 5.4 copy-start
  239.3 4.2 copy-start.5
  239.8 4.9 collective-permute-start
  247.0 3.3 copy-start.16
  250.3 18.3 %copy-start.10 = (f32[512,1024]{1,0:T(8,128)}, f32[512,1024]{1,0:T(8,128)S(1)}, u32[]{:S(2)}) copy-start(f32[512,1024]{1,0:T(8,128)S(1)} %get-tuple-element.51) | copy-start | bytes 6291460
  286.4 16.0 %copy-start.8 = (bf16[8,64,1024]{2,1,0:T(8,128)(2,1)S(1)}, bf16[8,64,1024]{2,1,0:T(8,128)(2,1)}, u32[]{:S(2)}) copy-start(bf16[8,64,1024]{2,1,0:T(8,128)(2,1)} %broadcast_select_fusion.2) | copy-start | bytes 3145732
  286.4 16.0 %copy-start.11 = (f32[512,1024]{1,0:T(8,128)S(1)}, f32[512,1024]{1,0:T(8,128)}, u32[]{:S(2)}) copy-start(f32[512,1024]{1,0:T(8,128)} %copy-done.10) | copy-start | bytes 6291460
  302.4 2.2 copy-start.17
  303.2 1.5 copy-start.2
  307.3 93.6 %reduce-scatter.6.cloned.1.call-start = ((), (), s32[]{:S(2)}) async-start(), calls=%async_computation.10 | async-start | bytes 7864320 | tf_op jit(solution)/shard_map/reduce_scatter | solution.py:156
  307.3 3.7 copy-start.1
  307.4 12.3 %slice-start = ((s8[6291456]{0:T(1024)(128)(4,1)}), s8[4194304]{0:T(1024)(128)(4,1)S(1)}, s32[]{:S(2)}) async-start(s8[6291456]{0:T(1024)(128)(4,1)} %bitcast.80), calls=%async_computation.17 | async-start | bytes 8388608
  311.0 8.6 slice-start.1
  313.4 9.4 copy-start.13
  313.5 5.8 collective-permute-start.1
  322.2 1.0 copy-start.14
  322.2 2.0 copy-start.19
  322.8 1.0 copy-start.15
  329.9 1.2 copy-start.9
  329.9 151.9 %reduce-scatter.12.cloned.1.call-start = ((), (), s32[]{:S(2)}) async-start(), calls=%async_computation.13 | async-start | bytes 11796480 | tf_op jit(solution)/shard_map/reduce_scatter | solution.py:165
  341.0 1.6 copy-start.12
  341.0 281.2 %reduce-scatter.10.cloned.1.call-start = ((), (), s32[]{:S(2)}) async-start(), calls=%async_computation.12 | async-start | bytes 23592960 | tf_op jit(solution)/shard_map/reduce_scatter | solution.py:162
  360.4 346.9 %reduce-scatter.14.cloned.1.call-start = ((), (), s32[]{:S(2)}) async-start(), calls=%async_computation.14 | async-start | bytes 20480 | tf_op jit(solution)/shard_map/reduce_scatter | solution.py:168
  370.7 610.2 %all-reduce.3.cloned.1.call-start = ((), (), s32[]{:S(2)}) async-start(), calls=%async_computation.16 | async-start | bytes 18350080 | tf_op jit(solution)/shard_map/psum | solution.py:176
  622.2 494.4 %all-gather.6.cloned.1.call-start = ((), (), s32[]{:S(2)}) async-start(), calls=%async_computation.15 | async-start | bytes 10321920 | tf_op jit(solution)/shard_map/all_gather | solution.py:203
  636.0 3.0 copy-start.3
  642.2 1.9 copy-start.4
  645.4 111.4 %copy-start.20 = (f32[5,256]{1,0:T(8,128)S(1)}, f32[5,256]{1,0:T(8,128)}, u32[]{:S(2)}) copy-start(f32[5,256]{1,0:T(8,128)} %param.19) | copy-start | bytes 15364
  703.6 54.7 %all-to-all-start.3 = ((bf16[8,64,1024]{2,1,0:T(8,128)(2,1)}), bf16[8,64,1024]{2,1,0:T(8,128)(2,1)S(1)}, u32[]{:S(2)}, u32[]{:S(2)}) async-start(bf16[8,64,1024]{2,1,0:T(8,128)(2,1)} %get-tuple-element.48), calls=%async_computation.3 | async-start | bytes 2097152 | tf_op jit(solution)/shard_map/all_to_all | solution.py:153
  758.3 222.7 %copy-start.6 = (bf16[8,64,1024]{2,1,0:T(8,128)(2,1)}, bf16[8,64,1024]{2,1,0:T(8,128)(2,1)S(1)}, u32[]{:S(2)}) copy-start(bf16[8,64,1024]{2,1,0:T(8,128)(2,1)S(1)} %all-to-all-done.3) | copy-start | bytes 3145732
  991.1 31.2 %slice-start.2 = ((s8[4587520]{0:T(1024)(128)(4,1)}), s8[393216]{0:T(1024)(128)(4,1)S(1)}, s32[]{:S(2)}) async-start(s8[4587520]{0:T(1024)(128)(4,1)} %bitcast.82), calls=%async_computation.19 | async-start | bytes 786432
  1010.3 12.0 %slice-start.3 = ((s8[4587520]{0:T(1024)(128)(4,1)}), s8[4194304]{0:T(1024)(128)(4,1)S(1)}, s32[]{:S(2)}) async-start(s8[4587520]{0:T(1024)(128)(4,1)} %bitcast.82), calls=%async_computation.20 | async-start | bytes 8388608
  1127.3 1.6 copy-start.7
Sparse Core Ops, SparseCore 0:
  9.6 224.1 all-gather.3
  307.4 31.9 reduce-scatter.7
  342.0 58.8 reduce-scatter.5
  403.9 77.9 reduce-scatter.11
  484.3 137.8 reduce-scatter.9
  625.0 19.4 reduce-scatter.13
  649.1 331.8 all-reduce.2
  983.0 133.6 all-gather.5
where the time goes:
time: 1140 us
  waiting for transfers between devices  689 us (60%)
  matrix products  212 us (19%)
  blocking collectives  118 us (10%)
  local copies, waits for them, and re-layouts  51.4 us (5%)
  other arithmetic  30.2 us (3%)
  starting transfers between devices  20.7 us (2%)
  between operations  14.9 us (1%)
    psum x1, waiting for transfers between devices, shards(): lax.psum(summed[3].astype(jnp.bfloat16), 'seq').astype(jnp.float32)  223 us
    all_gather x1, waiting for transfers between devices, shards(): lax.all_gather(weights, 'wsh', axis=0, tiled=True)  160 us
    reduce_scatter x1, waiting for transfers between devices, shards(): lax.psum_scatter(g_gu.astype(jnp.bfloat16), 'wsh', scatter_dimension=0, t...  140 us
    reduce_scatter x1, waiting for transfers between devices, shards(): lax.psum_scatter(g_down.astype(jnp.bfloat16), 'wsh', scatter_dimension=0,...  81 us
    all_to_all x1, blocking collectives, shards(): lax.all_to_all(leaving[0], 'seq', split_axis=0, concat_axis=0, tiled=True)  58.2 us
    psum x1, blocking collectives, shards(): lax.psum(summed[4].astype(jnp.bfloat16), 'seq').astype(jnp.float32)  49.4 us
    dot_general x4, matrix products, contract_cols(): lax.dot_general(left, right, (((1,), (1,)), ((), ())), preferred_element_...  39.1 us
    dot_general x4, matrix products, contract_rows(): lax.dot_general(left, right, (((0,), (0,)), ((), ())), preferred_element_...  36 us
  transfers between devices with their start and end apart: 13, of which 10 were waited for; matrix products, arithmetic and copies ran while one was open for 18% of the time, Pallas kernels for 0%

commit v1 on v0

--- a/solution.py
+++ b/solution.py
@@ -12,6 +12,27 @@
 LEARN = 0.03
 LEARN_VEC = 0.05
 HIGH = lax.Precision.HIGHEST
+
+
+def joined_along(blocks, dim):
+    blocks = jnp.moveaxis(blocks, 0, dim)
+    dims = blocks.shape
+    return blocks.reshape(*dims[:dim], dims[dim] * dims[dim + 1], *dims[dim + 2 :])
+
+
+def doubled(x, axis):
+    devices, place = (lax.axis_size(axis), lax.axis_index(axis))
+    parts, bit = (x[None], 1)
+    while bit < devices:
+        other = lax.ppermute(parts, axis, [(i, i ^ bit) for i in range(devices)])
+        low = place & bit == 0
+        parts = jnp.concatenate([jnp.where(low, parts, other), jnp.where(low, other, parts)])
+        bit *= 2
+    return parts
+
+
+def gather_by_bits(value, axis, dim):
+    return joined_along(doubled(value, axis), dim)
 
 
 def passed_along(block, axis, distance):
@@ -79,7 +100,7 @@
     x_bf = jnp.take(arrived[0], deal_order, axis=0).reshape(rows, D)
     dy_bf = jnp.take(arrived[1], deal_order, axis=0).reshape(rows, D)
     full_w, gains_bf, kernel_bf = (
-        lax.all_gather(weights, "wsh", axis=0, tiled=True),
+        gather_by_bits(weights, "wsh", 0),
         lax.all_gather(norm_gains, "wsh", axis=1, tiled=True),
         lax.all_gather(conv_kernel, "wsh", axis=1, tiled=True),
     )

time: 1140 us -> 1410 us (1.24)
  blocking collectives: 118 us -> 472 us
  waiting for transfers between devices: 689 us -> 533 us
  other arithmetic: 30.2 us -> 94.2 us
    all_gather x1, blocking collectives: 5.21 us -> 359 us  [shards(): lax.all_gather(norm_gains, 'wsh', axis=1, tiled=True)]
    all_gather x1 -> x0, waiting for transfers between devices: 160 us -> none  [shards(): lax.all_gather(weights, 'wsh', axis=0, tiled=True)]
    concatenate x0 -> x2, other arithmetic: none -> 35.4 us  [doubled(): jnp.concatenate([jnp.where(low, parts, other), jnp.where(low, other, part...]
    select_n x0 -> x2, other arithmetic: none -> 32 us  [doubled(): jnp.where(low, parts, other)]
    ppermute x0 -> x2, waiting for transfers between devices: none -> 14.3 us  [doubled(): other = lax.ppermute(parts, axis, [(i, i ^ bit) for i in range(devices)])]
  transfers between devices with their start and end apart: 13 -> 14, of which waited for: 10 -> 10; matrix products, arithmetic and copies ran while one was open for 18% -> 15% of each run, Pallas kernels for 0% -> 0%
where the time goes in v1:
time: 1410 us; the launch traced here: 1400 us
  waiting for transfers between devices  533 us (38%)
  blocking collectives  472 us (33%)
  matrix products  211 us (15%)
  other arithmetic  94.2 us (7%)
  local copies, waits for them, and re-layouts  51.5 us (4%)
  starting transfers between devices  23.3 us (2%)
  between operations  15 us (1%)
    all_gather x1, blocking collectives, shards(): lax.all_gather(norm_gains, 'wsh', axis=1, tiled=True)  359 us
    psum x1, waiting for transfers between devices, shards(): lax.psum(summed[3].astype(jnp.bfloat16), 'seq').astype(jnp.float32)  223 us
    reduce_scatter x1, waiting for transfers between devices, shards(): lax.psum_scatter(g_gu.astype(jnp.bfloat16), 'wsh', scatter_dimension=0, t...  140 us
    reduce_scatter x1, waiting for transfers between devices, shards(): lax.psum_scatter(g_down.astype(jnp.bfloat16), 'wsh', scatter_dimension=0,...  81.1 us
    all_to_all x1, blocking collectives, shards(): lax.all_to_all(leaving[0], 'seq', split_axis=0, concat_axis=0, tiled=True)  58.3 us
    psum x1, blocking collectives, shards(): lax.psum(summed[4].astype(jnp.bfloat16), 'seq').astype(jnp.float32)  49.4 us
    dot_general x4, matrix products, contract_cols(): lax.dot_general(left, right, (((1,), (1,)), ((), ())), preferred_element_...  39.4 us
    dot_general x4, matrix products, contract_rows(): lax.dot_general(left, right, (((0,), (0,)), ((), ())), preferred_element_...  35.7 us
  transfers between devices with their start and end apart: 14, of which 10 were waited for; matrix products, arithmetic and copies ran while one was open for 15% of the time, Pallas kernels for 0%

profile of v1, /device:TPU:0, one launch (start us, length us, event | category | flops | bytes accessed | tf_op | source)
XLA Modules:
  0.0 1400.6 jit_solution(8099678602235878044)
XLA Ops:
  7.7 14.3 %collective-permute-done = bf16[1,256,17920]{2,1,0:T(8,128)(2,1)} collective-permute-done((bf16[1,256,17920]{2,1,0:T(8,128)(2,1)}, bf16[1,256,17920]{2,1,0:T(8,128)(2,1)}, u32[]{:S(2)}, u32[]{:S(2)}) %collective-permute-start) | collective-permute-done | bytes 9175072 | tf_op jit(solution)/shard_map/ppermute | solution.py:27
  22.0 7.3 broadcast_select_fusion.3
  29.3 11.2 pad_maximum_fusion.1
  41.2 2.9 collective-permute-start.1
  44.0 5.8 all-to-all-start
  50.0 25.6 %all-to-all-done = bf16[8,64,1024]{2,1,0:T(8,128)(2,1)S(1)} async-done(((bf16[8,64,1024]{2,1,0:T(8,128)(2,1)}), bf16[8,64,1024]{2,1,0:T(8,128)(2,1)S(1)}, u32[]{:S(2)}, u32[]{:S(2)}) %all-to-all-start) | async-done | bytes 1048608 | tf_op jit(solution)/shard_map/all_to_all | solution.py:93
  75.6 4.2 all-to-all-start.2
  80.1 359.3 %all_gather.9 = bf16[2,1024]{1,0:T(2,128)(2,1)S(1)} all-gather(bf16[2,256]{1,0:T(2,128)(2,1)S(1)} %copy-done.28), channel_id=1, replica_groups=mesh['seq'=8,'wsh'=4] {'wsh'}, dimensions={1}, use_global_device_ids=true | all-gather | bytes 5120 | tf_op jit(solution)/shard_map/all_gather | solution.py:104
  439.4 5.2 all_gather.10
  445.9 1.8 gather_fusion.2
  448.1 24.7 %broadcast_select_fusion.1 = (bf16[2,256,17920]{2,1,0:T(8,128)(2,1)}, bf16[2,256,17920]{2,1,0:T(8,128)(2,1)}) fusion(bf16[2,256,17920]{2,1,0:T(8,128)(2,1)} %collective-permute-done.1, pred[]{:T(512)S(6)} %eq.6, bf16[1,256,17920]{2,1,0:T(8,128)(2,1)} %copy-done.1, bf16[1,256,17920]{2,1,0:T(8,128)(2,1)} %copy-done), kind=kLoop, calls=%fused_computation.10 | loop fusion | flops 27525120 | bytes 73400320 | tf_op jit(solution)/shard_map/jit(_where)/select_n | solution.py:29
  472.8 24.2 %pad_maximum_fusion = bf16[4,256,17920]{2,1,0:T(8,128)(2,1)} fusion(bf16[2,256,17920]{2,1,0:T(8,128)(2,1)} %get-tuple-element.32, bf16[2,256,17920]{2,1,0:T(8,128)(2,1)} %get-tuple-element.31), kind=kLoop, calls=%fused_computation.4 | loop fusion | flops 18350080 | bytes 73400320 | tf_op jit(solution)/shard_map/concatenate | solution.py:29
  497.0 5.5 fusion.14
  503.0 4.0 collective-permute-start.2
  507.9 2.3 multiply_convert_fusion.7
  510.3 3.3 multiply_reduce_fusion.3
  513.6 18.2 %fusion.4 = f32[512,9216]{1,0:T(8,128)} fusion(bf16[1024,17920]{1,0:T(8,128)(2,1)} %bitcast.86, f32[512,1024]{1,0:T(8,128)S(1)} %get-tuple-element.55, f32[1024]{0:T(1024)S(1)} %bitcast.112, f32[512]{0:T(512)S(1)} %add_rsqrt_fusion.1), kind=kOutput, calls=%fused_computation.14 | convolution fusion | flops 9665249280 | bytes 39852032 | tf_op jit(solution)/shard_map/dot_general | solution.py:131
  531.8 16.9 %multiply_convert_fusion.1 = (bf16[512,4608]{1,0:T(8,128)(2,1)}, bf16[512,4608]{1,0:T(8,128)(2,1)}, bf16[512,4608]{1,0:T(8,128)(2,1)}) fusion(f32[512,9216]{1,0:T(8,128)} %fusion.4, bf16[512,1024]{1,0:T(8,128)(2,1)S(1)} %bitcast.99, bf16[1024,17920]{1,0:T(8,128)(2,1)} %bitcast.87), kind=kOutput, calls=%fused_computation.19 | convolution fusion | flops 4869586944 | bytes 43515904 | tf_op jit(solution)/shard_map/dot_general | solution.py:139
  548.8 15.9 %multiply_reduce_fusion.1 = (bf16[1024]{0:T(1024)(128)(2,1)S(1)}, f32[512]{0:T(512)S(1)}, f32[512,1024]{1,0:T(8,128)S(1)}) fusion(f32[512,1024]{1,0:T(8,128)} %copy-done.12, f32[512]{0:T(512)S(1)} %add_rsqrt_fusion.1, f32[1024]{0:T(1024)S(1)} %bitcast.113, bf16[1024,17920]{1,0:T(8,128)(2,1)} %bitcast.88, bf16[512,4608]{1,0:T(8,128)(2,1)} %get-tuple-element.34, ...), kind=kOutput, calls=%fused_computation.81 | convolution fusion | flops 9685694464 | bytes 32516096 | tf_op jit(solution)/shard_map/dot_general | solution.py:71
  567.0 2.6 convolution_convert_fusion.3
  569.7 4.9 multiply_convert_fusion.4
  576.2 4.5 collective-permute-done.3
  581.1 2.6 fusion.26
  585.7 5.8 convolution_convert_fusion.2
  592.8 9.8 convolution_convert_fusion.1
  604.2 17.4 %convolution_convert_fusion = bf16[1024,9216]{1,0:T(8,128)(2,1)} fusion(bf16[512,4608]{1,0:T(8,128)(2,1)} %get-tuple-element.34, bf16[512,4608]{1,0:T(8,128)(2,1)} %get-tuple-element.33, f32[512,1024]{1,0:T(8,128)S(1)} %copy-done.14, f32[1024]{0:T(1024)S(1)} %bitcast.115, f32[512]{0:T(512)S(1)} %add_rsqrt_fusion.1), kind=kOutput, calls=%fused_computation.11 | convolution fusion | flops 9693560832 | bytes 30414848 | tf_op jit(solution)/shard_map/dot_general | solution.py:65
  622.3 8.8 fusion.41
  631.8 32.6 %reduce-scatter.6.cloned.1.call-done = bf16[256,3072]{1,0:T(8,128)(2,1)} async-done(((bf16[1024,3072]{1,0:T(8,128)(2,1)}), bf16[256,3072]{1,0:T(8,128)(2,1)}) %reduce-scatter.6.cloned.1.call-update) | async-done | bytes 1572880 | tf_op jit(solution)/shard_map/reduce_scatter | solution.py:177
  664.4 81.1 %reduce-scatter.12.cloned.1.call-done = bf16[256,4608]{1,0:T(8,128)(2,1)} async-done(((bf16[1024,4608]{1,0:T(8,128)(2,1)}), bf16[256,4608]{1,0:T(8,128)(2,1)}) %reduce-scatter.12.cloned.1.call-update) | async-done | bytes 2359312 | tf_op jit(solution)/shard_map/reduce_scatter | solution.py:186
  745.6 140.3 %reduce-scatter.10.cloned.1.call-done = bf16[256,9216]{1,0:T(8,128)(2,1)} async-done(((bf16[1024,9216]{1,0:T(8,128)(2,1)}), bf16[256,9216]{1,0:T(8,128)(2,1)}) %reduce-scatter.10.cloned.1.call-update) | async-done | bytes 4718608 | tf_op jit(solution)/shard_map/reduce_scatter | solution.py:183
  886.0 2.8 slice.250
  889.8 9.9 add_convert_fusion
  899.7 3.0 gather_fusion.1
  902.6 3.3 fusion.37
  905.9 1.9 gather_fusion.3
  909.1 58.3 %all_to_all.20 = bf16[8,64,1024]{2,1,0:T(8,128)(2,1)S(1)} all-to-all(bf16[8,64,1024]{2,1,0:T(8,128)(2,1)S(1)} %get-tuple-element.53), channel_id=1, replica_groups=mesh['seq'=8,'wsh'=4] {'seq'}, dimensions={0} | all-to-all | bytes 2097152 | tf_op jit(solution)/shard_map/all_to_all | solution.py:173
  967.4 3.7 all-to-all-start.3
  971.1 49.4 %psum.39 = bf16[5,256]{1,0:T(8,128)(2,1)S(1)} all-reduce(bf16[5,256]{1,0:T(8,128)(2,1)} %reduce-scatter.14.cloned.1.call-done), channel_id=1, replica_groups=mesh['seq'=8,'wsh'=4] {'seq'}, use_global_device_ids=true, to_apply=%region_21.23 | all-reduce | flops 1280 | bytes 5120 | tf_op jit(solution)/shard_map/psum | solution.py:198
  1022.0 222.6 %all-reduce.3.cloned.1.call-done = (bf16[256,4608]{1,0:T(8,128)(2,1)}, bf16[256,9216]{1,0:T(8,128)(2,1)}, bf16[256,1024]{1,0:T(8,128)(2,1)}, bf16[256,3072]{1,0:T(8,128)(2,1)}) async-done(((bf16[256,4608]{1,0:T(8,128)(2,1)}, bf16[256,9216]{1,0:T(8,128)(2,1)}, bf16[256,1024]{1,0:T(8,128)(2,1)}, bf16[256,3072]{1,0:T(8,128)(2,1)}), (bf16[256,4608]{1,0:T(8,128)(2,1)}, bf16[256,9216]{1,0:T(8,128)(2,1)}, ...) | async-done | bytes 9175056 | tf_op jit(solution)/shard_map/psum | solution.py:197
  1244.6 10.2 convert_multiply_fusion
  1254.8 19.2 %mul.433 = f32[2,128,140,128]{3,2,1,0:T(8,128)} reshape(f32[256,17920]{1,0:T(8,128)} %convert_multiply_fusion) | data formatting | bytes 36700160 | tf_op jit(solution)/shard_map/mul | solution.py:201
  1274.0 12.0 copy.22
  1286.0 29.5 %fusion.19 = f32[1,280,16,128]{3,2,1,0:T(8,128)S(1)} fusion(f32[2,280,16,128]{3,2,1,0:T(8,128)S(1)} %bitcast.95, f32[280,128,128]{2,1,0:T(8,128)S(1)} %bitcast.80, s32[]{:T(128)S(6)} %select_n.46), kind=kOutput, calls=%fused_computation.45 | convolution fusion | flops 882524160 | bytes 25231364 | tf_op jit(solution)/shard_map/nij,nkj->nik/dot_general | solution.py:216
  1315.5 35.2 %fusion.18 = f32[1,280,16,128]{3,2,1,0:T(8,128)S(1)} fusion(f32[2,280,16,128]{3,2,1,0:T(8,128)S(1)} %bitcast.95, f32[280,128,128]{2,1,0:T(8,128)S(1)} %bitcast.81, s32[]{:T(128)S(6)} %select_n.46), kind=kOutput, calls=%fused_computation.43 | convolution fusion | flops 882524160 | bytes 41287684 | tf_op jit(solution)/shard_map/nji,njk->nik/dot_general | solution.py:217
  1350.8 2.4 pad_maximum_fusion.5
  1353.2 17.0 %fusion.16 = f32[280,128,16]{1,2,0:T(8,128)S(1)} fusion(f32[280,128,128]{2,1,0:T(8,128)S(1)} %bitcast.82, f32[2,280,16,128]{3,2,1,0:T(8,128)} %param.21), kind=kOutput, calls=%fused_computation.40 | convolution fusion | flops 880803840 | bytes 22937600 | tf_op jit(solution)/shard_map/nij,njk->nik/dot_general | solution.py:227
  1370.2 10.2 all-gather.3.cloned.1.call-done
  1380.4 10.6 fusion.54
  (139 shorter events, 21.3 us)
Async XLA Ops:
  7.2 14.8 %collective-permute-start = (bf16[1,256,17920]{2,1,0:T(8,128)(2,1)}, bf16[1,256,17920]{2,1,0:T(8,128)(2,1)}, u32[]{:S(2)}, u32[]{:S(2)}) collective-permute-start(bf16[1,256,17920]{2,1,0:T(8,128)(2,1)} %bitcast.96), channel_id=1, source_target_pairs={{0,1},{1,0},{2,3},{3,2},{4,5},{5,4},{6,7},{7,6},{8,9},{9,8},{10,11... | collective-permute-start | bytes 27525128 | tf_op jit(solution)/shard_map/ppermute | solution.py:27
  29.3 11.2 copy-start
  29.3 11.9 copy-start.1
  29.3 20.6 %copy-start.29 = (s32[1,4]{1,0:T(1,128)S(1)}, s32[1,4]{1,0:T(1,128)}, u32[]{:S(2)}) copy-start(s32[1,4]{1,0:T(1,128)} %param.15) | copy-start | bytes 52
  41.2 38.9 %copy-start.28 = (bf16[2,256]{1,0:T(2,128)(2,1)S(1)}, bf16[2,256]{1,0:T(2,128)(2,1)}, u32[]{:S(2)}) copy-start(bf16[2,256]{1,0:T(2,128)(2,1)} %param.17) | copy-start | bytes 3076
  41.2 398.3 %copy-start.27 = (bf16[3,256]{1,0:T(4,128)(2,1)S(1)}, bf16[3,256]{1,0:T(4,128)(2,1)}, u32[]{:S(2)}) copy-start(bf16[3,256]{1,0:T(4,128)(2,1)} %param.18) | copy-start | bytes 4612
  41.2 403.5 %copy-start.30 = (s32[8]{0:T(128)S(1)}, s32[8]{0:T(128)}, u32[]{:S(2)}) copy-start(s32[8]{0:T(128)} %param.14) | copy-start | bytes 100
  41.2 406.9 %collective-permute-start.1 = (bf16[2,256,17920]{2,1,0:T(8,128)(2,1)}, bf16[2,256,17920]{2,1,0:T(8,128)(2,1)}, u32[]{:S(2)}, u32[]{:S(2)}) collective-permute-start(bf16[2,256,17920]{2,1,0:T(8,128)(2,1)} %pad_maximum_fusion.1), channel_id=1, source_target_pairs={{0,2},{1,3},{2,0},{3,1},{4,6},{5,7},{6,4},{7,5},{8,10},{9,11},{10,... | collective-permute-start | bytes 55050248 | tf_op jit(solution)/shard_map/ppermute | solution.py:27
  44.0 31.6 %all-to-all-start = ((bf16[8,64,1024]{2,1,0:T(8,128)(2,1)}), bf16[8,64,1024]{2,1,0:T(8,128)(2,1)S(1)}, u32[]{:S(2)}, u32[]{:S(2)}) async-start(bf16[8,64,1024]{2,1,0:T(8,128)(2,1)} %bitcast), calls=%async_computation | async-start | bytes 2097152 | tf_op jit(solution)/shard_map/all_to_all | solution.py:93
  75.6 370.2 %all-to-all-start.2 = ((bf16[8,64,1024]{2,1,0:T(8,128)(2,1)}), bf16[8,64,1024]{2,1,0:T(8,128)(2,1)}, u32[]{:S(2)}, u32[]{:S(2)}) async-start(bf16[8,64,1024]{2,1,0:T(8,128)(2,1)} %bitcast.12), calls=%async_computation.2 | async-start | bytes 2097152 | tf_op jit(solution)/shard_map/all_to_all | solution.py:96
  79.9 551.9 %reduce-scatter.8.cloned.1.call-start = ((), (), s32[]{:S(2)}) async-start(), calls=%async_computation.10 | async-start | bytes 2621440 | tf_op jit(solution)/shard_map/reduce_scatter | solution.py:180
  444.7 3.0 copy-start.22
  445.9 26.9 %copy-start.24 = (f32[512]{0:T(512)}, f32[512]{0:T(512)S(1)}, u32[]{:S(2)}) copy-start(f32[512]{0:T(512)S(1)} %rsqrt.23) | copy-start | bytes 6148
  448.1 49.0 %copy-start.19 = (bf16[512,1024]{1,0:T(8,128)(2,1)}, bf16[512,1024]{1,0:T(8,128)(2,1)S(1)}, u32[]{:S(2)}) copy-start(bf16[512,1024]{1,0:T(8,128)(2,1)S(1)} %fusion.32) | copy-start | bytes 3145732
  502.5 5.4 copy-start.2
  503.0 7.3 copy-start.3
  503.0 4.9 collective-permute-start.2
  507.2 57.5 %copy-start.10 = (bf16[8,64,1024]{2,1,0:T(8,128)(2,1)}, bf16[8,64,1024]{2,1,0:T(8,128)(2,1)S(1)}, u32[]{:S(2)}) copy-start(bf16[8,64,1024]{2,1,0:T(8,128)(2,1)S(1)} %broadcast_select_fusion.6) | copy-start | bytes 3145732
  510.3 3.3 copy-start.17
  513.6 18.2 %copy-start.12 = (f32[512,1024]{1,0:T(8,128)}, f32[512,1024]{1,0:T(8,128)S(1)}, u32[]{:S(2)}) copy-start(f32[512,1024]{1,0:T(8,128)S(1)} %get-tuple-element.55) | copy-start | bytes 6291460
  548.8 15.9 %copy-start.13 = (f32[512,1024]{1,0:T(8,128)S(1)}, f32[512,1024]{1,0:T(8,128)}, u32[]{:S(2)}) copy-start(f32[512,1024]{1,0:T(8,128)} %copy-done.12) | copy-start | bytes 6291460
  564.7 2.3 copy-start.18
  565.5 1.5 copy-start.5
  567.0 14.1 %slice-start = ((s8[6291456]{0:T(1024)(128)(4,1)}), s8[2097152]{0:T(1024)(128)(4,1)S(1)}, s32[]{:S(2)}) async-start(s8[6291456]{0:T(1024)(128)(4,1)} %bitcast.92), calls=%async_computation.16 | async-start | bytes 4194304
  569.6 94.8 %reduce-scatter.6.cloned.1.call-start = ((), (), s32[]{:S(2)}) async-start(), calls=%async_computation.9 | async-start | bytes 7864320 | tf_op jit(solution)/shard_map/reduce_scatter | solution.py:177
  569.7 11.4 slice-start.1
  574.6 9.6 copy-start.21
  574.6 6.5 copy-start.4
  574.7 6.1 collective-permute-start.3
  583.7 1.0 copy-start.15
  583.7 2.0 copy-start.20
  584.2 1.0 copy-start.16
  591.5 1.2 copy-start.11
  591.6 154.0 %reduce-scatter.12.cloned.1.call-start = ((), (), s32[]{:S(2)}) async-start(), calls=%async_computation.12 | async-start | bytes 11796480 | tf_op jit(solution)/shard_map/reduce_scatter | solution.py:186
  602.6 1.6 copy-start.14
  602.6 283.3 %reduce-scatter.10.cloned.1.call-start = ((), (), s32[]{:S(2)}) async-start(), calls=%async_computation.11 | async-start | bytes 23592960 | tf_op jit(solution)/shard_map/reduce_scatter | solution.py:183
  621.6 349.5 %reduce-scatter.14.cloned.1.call-start = ((), (), s32[]{:S(2)}) async-start(), calls=%async_computation.13 | async-start | bytes 20480 | tf_op jit(solution)/shard_map/reduce_scatter | solution.py:189
  631.7 612.9 %all-reduce.3.cloned.1.call-start = ((), (), s32[]{:S(2)}) async-start(), calls=%async_computation.15 | async-start | bytes 18350080 | tf_op jit(solution)/shard_map/psum | solution.py:197
  885.9 2.9 copy-start.31
  885.9 494.4 %all-gather.3.cloned.1.call-start = ((), (), s32[]{:S(2)}) async-start(), calls=%async_computation.14 | async-start | bytes 10321920 | tf_op jit(solution)/shard_map/all_gather | solution.py:224
  899.7 3.0 copy-start.6
  905.9 1.9 copy-start.7
  909.1 111.4 %copy-start.26 = (f32[5,256]{1,0:T(8,128)S(1)}, f32[5,256]{1,0:T(8,128)}, u32[]{:S(2)}) copy-start(f32[5,256]{1,0:T(8,128)} %param.19) | copy-start | bytes 15364
  967.4 54.7 %all-to-all-start.3 = ((bf16[8,64,1024]{2,1,0:T(8,128)(2,1)}), bf16[8,64,1024]{2,1,0:T(8,128)(2,1)S(1)}, u32[]{:S(2)}, u32[]{:S(2)}) async-start(bf16[8,64,1024]{2,1,0:T(8,128)(2,1)} %get-tuple-element.52), calls=%async_computation.3 | async-start | bytes 2097152 | tf_op jit(solution)/shard_map/all_to_all | solution.py:174
  1022.0 222.6 %copy-start.8 = (bf16[8,64,1024]{2,1,0:T(8,128)(2,1)}, bf16[8,64,1024]{2,1,0:T(8,128)(2,1)S(1)}, u32[]{:S(2)}) copy-start(bf16[8,64,1024]{2,1,0:T(8,128)(2,1)S(1)} %all-to-all-done.3) | copy-start | bytes 3145732
  1254.8 31.2 %slice-start.2 = ((s8[4587520]{0:T(1024)(128)(4,1)}), s8[393216]{0:T(1024)(128)(4,1)S(1)}, s32[]{:S(2)}) async-start(s8[4587520]{0:T(1024)(128)(4,1)} %bitcast.94), calls=%async_computation.18 | async-start | bytes 786432
  1274.0 12.0 slice-start.3
  1391.0 1.6 copy-start.9
  (2 other events, 1.4 us)
Sparse Core Ops, SparseCore 0:
  569.8 33.2 reduce-scatter.7
  605.6 58.8 reduce-scatter.5
  667.6 77.8 reduce-scatter.11
  748.0 137.8 reduce-scatter.9
  888.7 19.5 reduce-scatter.13
  912.7 331.8 all-reduce.2
  1246.7 133.6 all-gather.2
